TPU v7x, 32 devices: a whole 2x2x4 slice. The times are simulated.
32 devices in a mesh: rows: 8 (over z, x), tp: 2 (over core), job: 2 (over y).
Axes of the slice: x: 2, y: 2, z: 4, core: 2. Of those that a mesh axis runs over, the one named last changes fastest.
Arguments:
- train_query: bfloat16 [4096, 2048], P(('job', 'rows'), 'tp'), parts along dimension 0, may hold values from -0.125 to 0.125
- low_query: bfloat16 [4096, 16], P(('job', 'rows')), parts along dimension 0, may hold values from -0.125 to 0.125
- high_query: bfloat16 [32, 2048], P('job', 'tp'), parts along dimension 0, may hold values from -1.5 to 1.5
- train_key: bfloat16 [4096, 512], P(('job', 'rows'), 'tp'), parts along dimension 0, may hold values from -0.125 to 0.125
- low_key: bfloat16 [4096, 16], P(('job', 'rows')), parts along dimension 0, may hold values from -0.125 to 0.125
- high_key: bfloat16 [32, 512], P('job', 'tp'), parts along dimension 0, may hold values from -1.5 to 1.5
- train_value: bfloat16 [4096, 512], P(('job', 'rows'), 'tp'), parts along dimension 0, may hold values from -0.125 to 0.125
- low_value: bfloat16 [4096, 16], P(('job', 'rows')), parts along dimension 0, may hold values from -0.125 to 0.125
- high_value: bfloat16 [32, 512], P('job', 'tp'), parts along dimension 0, may hold values from -1.5 to 1.5
- norm_train: float32 [4096], P(('job', 'rows', 'tp')), parts along dimension 0, may hold values from 0.25 to 1.75
- norm_step: float32 [4096], P(('job', 'rows', 'tp')), parts along dimension 0, may hold values from -0.3 to 0.3
Outputs:
- serve_query: bfloat16 [4096, 2048], P(('job', 'tp')), parts along dimension 0
- serve_key: bfloat16 [1024, 2048], P(('job', 'tp')), parts along dimension 0
- serve_value: bfloat16 [1024, 2048], P(('job', 'tp')), parts along dimension 0
- serve_norm: bfloat16 [4096], P('job'), parts along dimension 0
There are 2 independent parts, one for each index of `job`. A program takes and returns all parts, laid end to end along the dimension named above; each array names one. Nothing has to cross between parts.
All inputs are finite; a program needn't handle non-finite values.
Results may differ from a plain program's by a relative error of at most 0.001.
Values may be sent and summed in bfloat16 or wider, within the bound.
A program may use at most 64 MiB of HBM per device.

v0:
```python
import functools

import jax
import jax.numpy as jnp
from jax import lax
from jax.experimental import pallas as pl
from jax.experimental.pallas import tpu as pltpu
from jax.sharding import PartitionSpec as P

mix_rate = 0.5
CHUNK_ROWS = 256
FIRST_ROWS = 256
VMEM_BYTES = 67043328
MESH = pl.DeviceIdType.MESH


def cuts(length, first):
    sizes = []
    while first and length > FIRST_ROWS and length % (2 * FIRST_ROWS) == 0:
        sizes.insert(0, min(length // 2, CHUNK_ROWS))
        length -= sizes[0]
    while length:
        sizes.insert(0, min(length, FIRST_ROWS if first else CHUNK_ROWS))
        length -= sizes[0]
    start, found = 0, []
    for rows in sizes:
        found.append((start, rows))
        start += rows
    return found


def kernel(
    size,
    tp_size,
    *refs,
):
    given, refs = refs[:11], refs[11:]
    serve_query, serve_key, serve_value, serve_norm = refs[:4]
    held, refs = refs[4:15], refs[15:]
    run_kernel(size, tp_size, given, held, serve_query, serve_key, serve_value, serve_norm, *refs)


def run_kernel(
    size,
    tp_size,
    given,
    held,
    serve_query,
    serve_key,
    serve_value,
    serve_norm,
    gains,
    load_sem,
    send_sem,
    recv_sem,
    gain_send,
    gain_recv,
):
    loads = [
        pltpu.make_async_copy(g, h, load_sem.at[n]) for n, (g, h) in enumerate(zip(given, held))
    ]
    (
        train_query,
        low_query,
        high_query,
        train_key,
        low_key,
        high_key,
        train_value,
        low_value,
        high_value,
        norm_train,
        norm_step,
    ) = held
    depth = size // 2
    me = lax.axis_index("rows")
    core = lax.axis_index("tp")
    z, x = me // 2, lax.rem(me, 2)
    other = 1 - x
    width = train_query.shape[0]
    up, down, side = me + 2, me - 2, 2 * z + other
    targets = (up, down, side)
    has_up, has_down = z < depth - 1, z > 0
    UP, DOWN, SIDE = 0, 1, 2

    def partner(k):
        return {"tp": lax.rem(core + k, tp_size)}

    barrier = pltpu.get_barrier_semaphore()

    def greet(device):
        pl.semaphore_signal(barrier, inc=1, device_id=device, device_id_type=MESH)

    @pl.when(has_up)
    def _():
        greet({"rows": up})

    @pl.when(has_down)
    def _():
        greet({"rows": down})

    greet({"rows": side})
    for k in range(1, tp_size):
        greet(partner(k))
    for load in loads:
        load.start()

    chunks = []
    for train, low, high, serve in (
        (train_query, low_query, high_query, serve_query),
        (train_key, low_key, high_key, serve_key),
        (train_value, low_value, high_value, serve_value),
    ):
        for start, rows in cuts(serve.shape[0], not chunks):
            chunks.append((train, low, high, serve, start, rows))
    count = len(chunks)
    queries = sum(c[3] is serve_query for c in chunks)
    twice, left = set(), sum(c[5] for c in chunks) // 2
    for c in sorted(range(count), key=lambda c: -chunks[c][5]):
        if chunks[c][5] <= left:
            twice.add(c)
            left -= chunks[c][5]

    def piece(item, c):
        if c == count:
            return gains.at[item]
        serve, start, rows = chunks[c][3:]
        return serve.at[pl.ds(start, rows), pl.ds(pl.multiple_of(item * width, 128), width)]

    def copy(item, c, way):
        ref = piece(item, c)
        return pltpu.make_async_remote_copy(
            src_ref=ref,
            dst_ref=ref,
            send_sem=send_sem.at[way, item, c],
            recv_sem=recv_sem.at[item, c],
            device_id={"rows": targets[way]},
            device_id_type=MESH,
        )

    def arrive(item, c):
        copy(item, c, SIDE).wait_recv()

    def crossing(c):
        return c in twice

    def merge(c):
        train, low, high, serve, start, length = chunks[c]
        rows = pl.ds(start, length)
        update = lax.dot_general(
            high[:, rows], low[...], (((0,), (0,)), ((), ())), preferred_element_type=jnp.float32
        )
        fresh = train[:, rows].T.astype(jnp.float32) + mix_rate * update
        serve[rows, pl.ds(pl.multiple_of(me * width, 128), width)] = fresh.astype(jnp.bfloat16)

    def send_own(c):
        @pl.when(has_down)
        def _():
            copy(me, c, DOWN).start()

        @pl.when(has_up)
        def _():
            copy(me, c, UP).start()

        copy(me, c, SIDE).start()

    def gain_copy(k):
        return pltpu.make_async_remote_copy(
            src_ref=gains.at[me, core],
            dst_ref=gains.at[me, core],
            send_sem=gain_send.at[k],
            recv_sem=gain_recv.at[k],
            device_id=partner(k),
            device_id_type=MESH,
        )

    for n in (0, 1, 2, 9, 10):
        loads[n].wait()
    gains[pl.ds(me, 1), pl.ds(core, 1)] = (norm_train[...] + norm_step[...])[None, None]
    merge(0)
    merge(1)
    pl.semaphore_wait(barrier, tp_size + has_up.astype(jnp.int32) + has_down.astype(jnp.int32))
    for c in range(2, count + 2):
        send_own(c - 2)
        if c < count:
            if c == queries:
                for n in range(3, 9):
                    loads[n].wait()
            merge(c)
        if c == 3:
            for k in range(1, tp_size):
                gain_copy(k).start()
    for k in range(1, tp_size):
        gain_copy(k).wait_recv()
    send_own(count)

    def pass_on(step, c):
        below, above = me - 2 * step, me + 2 * step

        @pl.when(z >= step)
        def _():
            arrive(below, c)

            @pl.when(has_up)
            def _():
                copy(below, c, UP).start()

            if not (step == 1 and crossing(c)):
                copy(below, c, SIDE).start()

        @pl.when(z + step < depth)
        def _():
            arrive(above, c)

            @pl.when(has_down)
            def _():
                copy(above, c, DOWN).start()

            if not (step == 1 and crossing(c)):
                copy(above, c, SIDE).start()

    def cross(c):
        arrive(side, c)

        @pl.when(has_down)
        def _():
            copy(side, c, DOWN).start()

        @pl.when(has_up)
        def _():
            copy(side, c, UP).start()

    for step in range(1, depth):
        for c in range(count + 1):
            pass_on(step, c)
        if step == max(1, depth - 2):
            for c in range(count):
                if crossing(c):
                    cross(c)

    for c in range(count + 1):
        if not crossing(c):
            arrive(side, c)
    for step in range(1, depth):
        for c in range(count + 1):
            @pl.when(z >= step)
            def _():
                arrive(side - 2 * step, c)

            @pl.when(z + step < depth)
            def _():
                arrive(side + 2 * step, c)

    serve_norm[...] = gains[...].reshape(serve_norm.shape).astype(jnp.bfloat16)

    for k in range(1, tp_size):
        gain_copy(k).wait_send()
    for c in range(count + 1):
        copy(me, c, SIDE).wait_send()

        @pl.when(has_down)
        def _():
            copy(me, c, DOWN).wait_send()
            if crossing(c):
                copy(side, c, DOWN).wait_send()

        @pl.when(has_up)
        def _():
            copy(me, c, UP).wait_send()
            if crossing(c):
                copy(side, c, UP).wait_send()

        for step in range(1, depth):
            below, above = me - 2 * step, me + 2 * step

            @pl.when(z >= step)
            def _():
                @pl.when(has_up)
                def _():
                    copy(below, c, UP).wait_send()

                if not (step == 1 and crossing(c)):
                    copy(below, c, SIDE).wait_send()

            @pl.when(z + step < depth)
            def _():
                @pl.when(has_down)
                def _():
                    copy(above, c, DOWN).wait_send()

                if not (step == 1 and crossing(c)):
                    copy(above, c, SIDE).wait_send()


def fused(size, tp_size, *args):
    train_query, train_key, train_value, norm_train = args[0], args[3], args[6], args[9]
    seats, norm_length = size * tp_size, norm_train.shape[0]
    args = [a.T if n in (1, 4, 7) else a for n, a in enumerate(args)]
    args = [a.reshape(1, -1) if a.ndim == 1 else a for a in args]
    full = train_query.shape[0] * size
    outs = [
        pltpu.VMEM((t.shape[1], full), jnp.bfloat16)
        for t in (train_query, train_key, train_value)
    ]
    outs.append(pltpu.VMEM((seats, norm_length), jnp.bfloat16))
    lengths = [t.shape[1] for t in (train_query, train_key, train_value)]
    count = sum(len(cuts(length, n == 0)) for n, length in enumerate(lengths))
    grant = VMEM_BYTES - 2 * (sum(t.shape[1] for t in (train_query, train_key, train_value)) * full)
    grant -= 2 * seats * norm_length
    vmem = pl.BlockSpec(memory_space=pltpu.VMEM)
    query, key, value, norm = pl.pallas_call(
        functools.partial(kernel, size, tp_size),
        out_shape=outs,
        in_specs=[pl.BlockSpec(memory_space=pltpu.HBM)] * 11,
        out_specs=[vmem] * 4,
        scratch_shapes=[pltpu.VMEM(a.shape, a.dtype) for a in args]
        + [
            pltpu.VMEM((size, tp_size, 1, norm_length), jnp.float32),
            pltpu.SemaphoreType.DMA((11,)),
            pltpu.SemaphoreType.DMA((3, size, count + 1)),
            pltpu.SemaphoreType.DMA((size, count + 1)),
            pltpu.SemaphoreType.DMA((tp_size,)),
            pltpu.SemaphoreType.DMA((tp_size,)),
        ],
        compiler_params=pltpu.CompilerParams(
            collective_id=0, has_side_effects=True, vmem_limit_bytes=grant
        ),
    )(*args)
    query, key, value, norm = store_out(query, key, value, norm)
    return query, key, value, norm.reshape(-1)


def store_kernel(*refs):
    ins, outs, sems = refs[:4], refs[4:8], refs[8]
    copies = [pltpu.make_async_copy(i, o, sems.at[n]) for n, (i, o) in enumerate(zip(ins, outs))]
    for c in copies:
        c.start()
    for c in copies:
        c.wait()


def store_out(*arrays):
    return pl.pallas_call(
        store_kernel,
        out_shape=[jax.ShapeDtypeStruct(a.shape, a.dtype) for a in arrays],
        in_specs=[pl.BlockSpec(memory_space=pltpu.VMEM)] * 4,
        out_specs=[pl.BlockSpec(memory_space=pltpu.HBM)] * 4,
        scratch_shapes=[pltpu.SemaphoreType.DMA((4,))],
        compiler_params=pltpu.CompilerParams(vmem_limit_bytes=16 * 2**20),
    )(*arrays)


def plain(
    train_query,
    low_query,
    high_query,
    train_key,
    low_key,
    high_key,
    train_value,
    low_value,
    high_value,
    norm_train,
    norm_step,
):
    def merged(train, low, high):
        update = jnp.dot(low, high, preferred_element_type=jnp.float32)
        fresh = train.astype(jnp.float32) + mix_rate * update
        return lax.all_gather(fresh.astype(jnp.bfloat16), "rows", axis=0, tiled=True).T

    serve_norm = lax.all_gather(
        (norm_train + norm_step).astype(jnp.bfloat16), ("rows", "tp"), axis=0, tiled=True
    )
    return (
        merged(train_query, low_query, high_query),
        merged(train_key, low_key, high_key),
        merged(train_value, low_value, high_value),
        serve_norm,
    )


def solution(mesh):
    size, tp_size = mesh.shape["rows"], mesh.shape["tp"]

    def local(*args):
        trains = (args[0], args[3], args[6])
        fits = (
            size % 2 == 0
            and size >= 4
            and all(t.shape[0] % 128 == 0 and t.shape[1] % FIRST_ROWS == 0 for t in trains)
            and args[9].shape[0] % 128 == 0
        )
        return fused(size, tp_size, *args) if fits else plain(*args)

    in_specs = (
        P(("job", "rows"), "tp"),
        P(("job", "rows"), None),
        P("job", "tp"),
        P(("job", "rows"), "tp"),
        P(("job", "rows"), None),
        P("job", "tp"),
        P(("job", "rows"), "tp"),
        P(("job", "rows"), None),
        P("job", "tp"),
        P(("job", "rows", "tp")),
        P(("job", "rows", "tp")),
    )
    out_specs = (P(("job", "tp"), None), P(("job", "tp"), None), P(("job", "tp"), None), P("job"))
    return jax.shard_map(local, mesh=mesh, in_specs=in_specs, out_specs=out_specs, check_vma=False)
```

profile of v0, /device:TPU:0, one launch (start us, length us, event | category | flops | bytes accessed | tf_op | source)
XLA Modules:
  0.0 69.8 jit_solution(11022188700209379372)
XLA Ops:
  0.6 66.5 %shard_map.138 = (bf16[1024,2048]{1,0:T(8,128)(2,1)S(1)}, bf16[256,2048]{1,0:T(8,128)(2,1)S(1)}, bf16[256,2048]{1,0:T(8,128)(2,1)S(1)}, bf16[16,128]{1,0:T(8,128)(2,1)S(1)}) custom-call(bf16[256,1024]{1,0:T(8,128)(2,1)} %refs_0_.1, bf16[16,256]{1,0:T(8,128)(2,1)} %bitcast.6, bf16[16,1024]{1,0:T(8,128)(2,1)} %refs_2_.1, bf16[256,256]{1,0:T(8,128)(2,1)} %refs_3_.1, ...), custom_call_target="tpu_custom_call" | custom-call | tf_op jit(solution)/shard_map/pallas_call | solution.py:311
  67.1 2.7 %shard_map.139 = (bf16[1024,2048]{1,0:T(8,128)(2,1)}, bf16[256,2048]{1,0:T(8,128)(2,1)}, bf16[256,2048]{1,0:T(8,128)(2,1)}, bf16[16,128]{1,0:T(8,128)(2,1)}) custom-call(bf16[1024,2048]{1,0:T(8,128)(2,1)S(1)} %get-tuple-element.12.refs_0_, bf16[256,2048]{1,0:T(8,128)(2,1)S(1)} %get-tuple-element.13.refs_1_, bf16[256,2048]{1,0:T(8,128)(2,1)S(1)} %get-tuple-element.14.refs_2_, ...), custom_call_target="tpu_custom_call" | custom-call | tf_op jit(solution)/shard_map/pallas_call | solution.py:343
where the time goes:
time: 70 us; the launch traced here: 69.8 us
  Pallas kernels  69.2 us (99%)
    pallas_call x1, Pallas kernels, fused(): pl.pallas_call(functools.partial(kernel, size, tp_size), out_shape=outs,...  66.5 us
    pallas_call x1, Pallas kernels, store_out(): pl.pallas_call(store_kernel, out_shape=[jax.ShapeDtypeStruct(a.shape, a.d...  2.71 us

commit v1 on v0

--- a/solution.py
+++ b/solution.py
@@ -52,9 +52,14 @@
     gains,
     load_sem,
     send_sem,
-    recv_sem,
+    line_sem,
+    cross_sem,
+    rest_sem,
     gain_send,
-    gain_recv,
+    gain_line,
+    gain_rest,
+    pair_send,
+    pair_recv,
 ):
     loads = [
         pltpu.make_async_copy(g, h, load_sem.at[n]) for n, (g, h) in enumerate(zip(given, held))
@@ -121,25 +126,54 @@
             twice.add(c)
             left -= chunks[c][5]
 
+    crossings = sorted(twice)
+    tall = sum(c[5] for c in chunks)
+    cross_tall = sum(chunks[c][5] for c in crossings)
+
     def piece(item, c):
         if c == count:
             return gains.at[item]
         serve, start, rows = chunks[c][3:]
         return serve.at[pl.ds(start, rows), pl.ds(pl.multiple_of(item * width, 128), width)]
 
-    def copy(item, c, way):
+    def landing(item, c, way, own_side):
+        if c == count:
+            return gain_rest.at[0] if way == SIDE else gain_line.at[item // 2]
+        if way != SIDE:
+            return line_sem.at[item // 2, c]
+        if own_side and crossing(c):
+            return cross_sem.at[crossings.index(c)]
+        return rest_sem.at[0]
+
+    def copy(item, c, way, recv):
         ref = piece(item, c)
         return pltpu.make_async_remote_copy(
             src_ref=ref,
             dst_ref=ref,
-            send_sem=send_sem.at[way, item, c],
-            recv_sem=recv_sem.at[item, c],
+            send_sem=gain_send.at[way] if c == count else send_sem.at[way],
+            recv_sem=recv,
             device_id={"rows": targets[way]},
             device_id_type=MESH,
         )
 
-    def arrive(item, c):
-        copy(item, c, SIDE).wait_recv()
+    def send(item, c, way, own=False):
+        copy(item, c, way, landing(item, c, way, own)).start()
+
+    def arrive_line(item, c):
+        copy(item, c, UP, landing(item, c, UP, False)).wait_recv()
+
+    def bulk(ref, send, recv):
+        return pltpu.make_async_remote_copy(
+            src_ref=ref,
+            dst_ref=ref,
+            send_sem=send,
+            recv_sem=recv,
+            device_id={"rows": side},
+            device_id_type=MESH,
+        )
+
+    def span(rows):
+        return serve_query.at[pl.ds(0, rows // size), :]
 
     def crossing(c):
         return c in twice
@@ -156,20 +190,20 @@
     def send_own(c):
         @pl.when(has_down)
         def _():
-            copy(me, c, DOWN).start()
+            send(me, c, DOWN)
 
         @pl.when(has_up)
         def _():
-            copy(me, c, UP).start()
-
-        copy(me, c, SIDE).start()
+            send(me, c, UP)
+
+        send(me, c, SIDE, own=True)
 
     def gain_copy(k):
         return pltpu.make_async_remote_copy(
             src_ref=gains.at[me, core],
             dst_ref=gains.at[me, core],
-            send_sem=gain_send.at[k],
-            recv_sem=gain_recv.at[k],
+            send_sem=pair_send.at[k],
+            recv_sem=pair_recv.at[k],
             device_id=partner(k),
             device_id_type=MESH,
         )
@@ -199,97 +233,67 @@
 
         @pl.when(z >= step)
         def _():
-            arrive(below, c)
+            arrive_line(below, c)
 
             @pl.when(has_up)
             def _():
-                copy(below, c, UP).start()
+                send(below, c, UP)
 
             if not (step == 1 and crossing(c)):
-                copy(below, c, SIDE).start()
+                send(below, c, SIDE)
 
         @pl.when(z + step < depth)
         def _():
-            arrive(above, c)
+            arrive_line(above, c)
 
             @pl.when(has_down)
             def _():
-                copy(above, c, DOWN).start()
+                send(above, c, DOWN)
 
             if not (step == 1 and crossing(c)):
-                copy(above, c, SIDE).start()
+                send(above, c, SIDE)
 
     def cross(c):
-        arrive(side, c)
+        copy(side, c, SIDE, landing(side, c, SIDE, True)).wait_recv()
 
         @pl.when(has_down)
         def _():
-            copy(side, c, DOWN).start()
+            copy(side, c, DOWN, rest_sem.at[0]).start()
 
         @pl.when(has_up)
         def _():
-            copy(side, c, UP).start()
+            copy(side, c, UP, rest_sem.at[0]).start()
 
     for step in range(1, depth):
         for c in range(count + 1):
             pass_on(step, c)
         if step == max(1, depth - 2):
-            for c in range(count):
-                if crossing(c):
-                    cross(c)
-
-    for c in range(count + 1):
-        if not crossing(c):
-            arrive(side, c)
-    for step in range(1, depth):
-        for c in range(count + 1):
-            @pl.when(z >= step)
-            def _():
-                arrive(side - 2 * step, c)
-
-            @pl.when(z + step < depth)
-            def _():
-                arrive(side + 2 * step, c)
-
+            for c in crossings:
+                cross(c)
+
+    bulk(gains.at[pl.ds(0, depth)], gain_send.at[SIDE], gain_rest.at[0]).wait()
     serve_norm[...] = gains[...].reshape(serve_norm.shape).astype(jnp.bfloat16)
+    bulk(span(depth * tall - cross_tall), send_sem.at[SIDE], rest_sem.at[0]).wait_recv()
 
     for k in range(1, tp_size):
         gain_copy(k).wait_send()
-    for c in range(count + 1):
-        copy(me, c, SIDE).wait_send()
-
-        @pl.when(has_down)
-        def _():
-            copy(me, c, DOWN).wait_send()
-            if crossing(c):
-                copy(side, c, DOWN).wait_send()
-
-        @pl.when(has_up)
-        def _():
-            copy(me, c, UP).wait_send()
-            if crossing(c):
-                copy(side, c, UP).wait_send()
-
-        for step in range(1, depth):
-            below, above = me - 2 * step, me + 2 * step
-
-            @pl.when(z >= step)
-            def _():
-                @pl.when(has_up)
-                def _():
-                    copy(below, c, UP).wait_send()
-
-                if not (step == 1 and crossing(c)):
-                    copy(below, c, SIDE).wait_send()
-
-            @pl.when(z + step < depth)
-            def _():
-                @pl.when(has_down)
-                def _():
-                    copy(above, c, DOWN).wait_send()
-
-                if not (step == 1 and crossing(c)):
-                    copy(above, c, SIDE).wait_send()
+    for level in range(depth):
+        up_rows = ((level + 1) * tall + cross_tall) if level < depth - 1 else 0
+        down_rows = ((depth - level) * tall + cross_tall) if level else 0
+        ends = (level > 0) + (level < depth - 1)
+
+        @pl.when(z == level)
+        def _():
+            bulk(span(depth * tall - ends * cross_tall), send_sem.at[SIDE], rest_sem.at[0]).wait_send()
+            for way, rows, items in (
+                (UP, up_rows, level + 1),
+                (DOWN, down_rows, depth - level),
+            ):
+                if rows:
+                    bulk(span(rows), send_sem.at[way], rest_sem.at[0]).wait_send()
+                    bulk(
+                        gains.at[pl.ds(0, items)], gain_send.at[way], gain_rest.at[0]
+                    ).wait_send()
 
 
 def fused(size, tp_size, *args):
@@ -317,8 +321,13 @@
         + [
             pltpu.VMEM((size, tp_size, 1, norm_length), jnp.float32),
             pltpu.SemaphoreType.DMA((11,)),
-            pltpu.SemaphoreType.DMA((3, size, count + 1)),
-            pltpu.SemaphoreType.DMA((size, count + 1)),
+            pltpu.SemaphoreType.DMA((3,)),
+            pltpu.SemaphoreType.DMA((size // 2, count)),
+            pltpu.SemaphoreType.DMA((count,)),
+            pltpu.SemaphoreType.DMA((1,)),
+            pltpu.SemaphoreType.DMA((3,)),
+            pltpu.SemaphoreType.DMA((size // 2,)),
+            pltpu.SemaphoreType.DMA((1,)),
             pltpu.SemaphoreType.DMA((tp_size,)),
             pltpu.SemaphoreType.DMA((tp_size,)),
         ],

time: 70 us -> 68.2 us (0.974)
  Pallas kernels: 69.2 us -> 67.4 us
    pallas_call x1, Pallas kernels: 66.5 us -> 64.7 us  [fused(): pl.pallas_call(functools.partial(kernel, size, tp_size), out_shape=outs,...]
where the time goes in v1:
time: 68.2 us; the launch traced here: 68.1 us
  Pallas kernels  67.4 us (99%)
    pallas_call x1, Pallas kernels, fused(): pl.pallas_call(functools.partial(kernel, size, tp_size), out_shape=outs,...  64.7 us
    pallas_call x1, Pallas kernels, store_out(): pl.pallas_call(store_kernel, out_shape=[jax.ShapeDtypeStruct(a.shape, a.d...  2.71 us

profile of v1, /device:TPU:0, one launch (start us, length us, event | category | flops | bytes accessed | tf_op | source)
XLA Modules:
  0.0 68.1 jit_solution(3514044745793514059)
XLA Ops:
  0.6 64.7 %shard_map.138 = (bf16[1024,2048]{1,0:T(8,128)(2,1)S(1)}, bf16[256,2048]{1,0:T(8,128)(2,1)S(1)}, bf16[256,2048]{1,0:T(8,128)(2,1)S(1)}, bf16[16,128]{1,0:T(8,128)(2,1)S(1)}) custom-call(bf16[256,1024]{1,0:T(8,128)(2,1)} %refs_0_.1, bf16[16,256]{1,0:T(8,128)(2,1)} %bitcast.6, bf16[16,1024]{1,0:T(8,128)(2,1)} %refs_2_.1, bf16[256,256]{1,0:T(8,128)(2,1)} %refs_3_.1, ...), custom_call_target="tpu_custom_call" | custom-call | tf_op jit(solution)/shard_map/pallas_call | solution.py:315
  65.4 2.7 %shard_map.139 = (bf16[1024,2048]{1,0:T(8,128)(2,1)}, bf16[256,2048]{1,0:T(8,128)(2,1)}, bf16[256,2048]{1,0:T(8,128)(2,1)}, bf16[16,128]{1,0:T(8,128)(2,1)}) custom-call(bf16[1024,2048]{1,0:T(8,128)(2,1)S(1)} %get-tuple-element.12.refs_0_, bf16[256,2048]{1,0:T(8,128)(2,1)S(1)} %get-tuple-element.13.refs_1_, bf16[256,2048]{1,0:T(8,128)(2,1)S(1)} %get-tuple-element.14.refs_2_, ...), custom_call_target="tpu_custom_call" | custom-call | tf_op jit(solution)/shard_map/pallas_call | solution.py:352

commit v2 on v1

--- a/solution.py
+++ b/solution.py
@@ -9,24 +9,32 @@
 
 mix_rate = 0.5
 CHUNK_ROWS = 256
-FIRST_ROWS = 256
+SMALL_ROWS = 128
+RELIEF = 1
 VMEM_BYTES = 67043328
 MESH = pl.DeviceIdType.MESH
 
 
 def cuts(length, first):
-    sizes = []
-    while first and length > FIRST_ROWS and length % (2 * FIRST_ROWS) == 0:
-        sizes.insert(0, min(length // 2, CHUNK_ROWS))
-        length -= sizes[0]
+    sizes = [SMALL_ROWS] * 2 if first else []
+    length -= sum(sizes)
     while length:
-        sizes.insert(0, min(length, FIRST_ROWS if first else CHUNK_ROWS))
-        length -= sizes[0]
+        sizes.append(min(length, CHUNK_ROWS))
+        length -= sizes[-1]
     start, found = 0, []
     for rows in sizes:
         found.append((start, rows))
         start += rows
     return found
+
+
+def crossed(rows):
+    twice, left = [], sum(rows) // 2
+    for c in sorted(range(len(rows)), key=lambda c: -rows[c]):
+        if c != RELIEF and rows[c] <= left:
+            twice.append(c)
+            left -= rows[c]
+    return sorted(twice)
 
 
 def kernel(
@@ -60,6 +68,8 @@
     gain_rest,
     pair_send,
     pair_recv,
+    stage,
+    stage_sem,
 ):
     loads = [
         pltpu.make_async_copy(g, h, load_sem.at[n]) for n, (g, h) in enumerate(zip(given, held))
@@ -107,6 +117,19 @@
     greet({"rows": side})
     for k in range(1, tp_size):
         greet(partner(k))
+    job = lax.axis_index("job")
+    near = (core == 0) & ((me == 1) | (me == 2))
+    source, helper = near & (job == 0), near & (job == 1)
+
+    @pl.when((core == 0) & (me == 0) & (job == 0))
+    def _():
+        for row in (1, 2):
+            greet({"job": 1, "rows": row})
+
+    @pl.when(helper)
+    def _():
+        greet({"job": 0})
+
     for load in loads:
         load.start()
 
@@ -120,13 +143,7 @@
             chunks.append((train, low, high, serve, start, rows))
     count = len(chunks)
     queries = sum(c[3] is serve_query for c in chunks)
-    twice, left = set(), sum(c[5] for c in chunks) // 2
-    for c in sorted(range(count), key=lambda c: -chunks[c][5]):
-        if chunks[c][5] <= left:
-            twice.add(c)
-            left -= chunks[c][5]
-
-    crossings = sorted(twice)
+    crossings = crossed([c[5] for c in chunks])
     tall = sum(c[5] for c in chunks)
     cross_tall = sum(chunks[c][5] for c in crossings)
 
@@ -150,7 +167,7 @@
         return pltpu.make_async_remote_copy(
             src_ref=ref,
             dst_ref=ref,
-            send_sem=gain_send.at[way] if c == count else send_sem.at[way],
+            send_sem=gain_send.at[0] if c == count else send_sem.at[way],
             recv_sem=recv,
             device_id={"rows": targets[way]},
             device_id_type=MESH,
@@ -176,7 +193,7 @@
         return serve_query.at[pl.ds(0, rows // size), :]
 
     def crossing(c):
-        return c in twice
+        return c in crossings
 
     def merge(c):
         train, low, high, serve, start, length = chunks[c]
@@ -188,7 +205,15 @@
         serve[rows, pl.ds(pl.multiple_of(me * width, 128), width)] = fresh.astype(jnp.bfloat16)
 
     def send_own(c):
-        @pl.when(has_down)
+        down, across = has_down, True
+        if c == RELIEF:
+            down, across = has_down & ~(source & (me == 2)), ~(source & (me == 1))
+
+            @pl.when(source)
+            def _():
+                hand_over().start()
+
+        @pl.when(down)
         def _():
             send(me, c, DOWN)
 
@@ -196,14 +221,36 @@
         def _():
             send(me, c, UP)
 
-        send(me, c, SIDE, own=True)
+        @pl.when(across)
+        def _():
+            send(me, c, SIDE, own=True)
+
+    def hand_over():
+        return pltpu.make_async_remote_copy(
+            src_ref=piece(me, RELIEF),
+            dst_ref=stage,
+            send_sem=stage_sem.at[0],
+            recv_sem=stage_sem.at[1],
+            device_id={"job": 1},
+            device_id_type=MESH,
+        )
+
+    def relieve(way):
+        return pltpu.make_async_remote_copy(
+            src_ref=stage,
+            dst_ref=piece(me, RELIEF),
+            send_sem=stage_sem.at[2],
+            recv_sem=landing(me, RELIEF, way, True),
+            device_id={"job": 0, "rows": 0},
+            device_id_type=MESH,
+        )
 
     def gain_copy(k):
         return pltpu.make_async_remote_copy(
             src_ref=gains.at[me, core],
             dst_ref=gains.at[me, core],
-            send_sem=pair_send.at[k],
-            recv_sem=pair_recv.at[k],
+            send_sem=pair_send.at[k - 1],
+            recv_sem=pair_recv.at[k - 1],
             device_id=partner(k),
             device_id_type=MESH,
         )
@@ -213,7 +260,8 @@
     gains[pl.ds(me, 1), pl.ds(core, 1)] = (norm_train[...] + norm_step[...])[None, None]
     merge(0)
     merge(1)
-    pl.semaphore_wait(barrier, tp_size + has_up.astype(jnp.int32) + has_down.astype(jnp.int32))
+    expected = sum(e.astype(jnp.int32) for e in (has_up, has_down, source, helper))
+    pl.semaphore_wait(barrier, tp_size + expected)
     for c in range(2, count + 2):
         send_own(c - 2)
         if c < count:
@@ -228,6 +276,18 @@
         gain_copy(k).wait_recv()
     send_own(count)
 
+    @pl.when(helper)
+    def _():
+        hand_over().wait_recv()
+
+        @pl.when(me == 1)
+        def _():
+            relieve(SIDE).start()
+
+        @pl.when(me == 2)
+        def _():
+            relieve(DOWN).start()
+
     def pass_on(step, c):
         below, above = me - 2 * step, me + 2 * step
 
@@ -264,36 +324,57 @@
         def _():
             copy(side, c, UP, rest_sem.at[0]).start()
 
+    order = [c for c in range(count + 1) if c != RELIEF] + [RELIEF]
     for step in range(1, depth):
-        for c in range(count + 1):
+        for c in order:
             pass_on(step, c)
         if step == max(1, depth - 2):
             for c in crossings:
                 cross(c)
 
-    bulk(gains.at[pl.ds(0, depth)], gain_send.at[SIDE], gain_rest.at[0]).wait()
-    serve_norm[...] = gains[...].reshape(serve_norm.shape).astype(jnp.bfloat16)
+    bulk(gains.at[pl.ds(0, depth)], gain_send.at[0], gain_rest.at[0]).wait_recv()
+    serve_norm[...] = gains[:size].reshape(serve_norm.shape).astype(jnp.bfloat16)
     bulk(span(depth * tall - cross_tall), send_sem.at[SIDE], rest_sem.at[0]).wait_recv()
 
     for k in range(1, tp_size):
         gain_copy(k).wait_send()
+    @pl.when(source)
+    def _():
+        hand_over().wait_send()
+
+    @pl.when(helper)
+    def _():
+        relieve(SIDE).wait_send()
+
     for level in range(depth):
-        up_rows = ((level + 1) * tall + cross_tall) if level < depth - 1 else 0
-        down_rows = ((depth - level) * tall + cross_tall) if level else 0
-        ends = (level > 0) + (level < depth - 1)
+        has = {UP: level < depth - 1, DOWN: level > 0, SIDE: True}
+        rows = {
+            UP: (level + 1) * tall + cross_tall,
+            DOWN: (depth - level) * tall + cross_tall,
+            SIDE: depth * tall - (has[UP] + has[DOWN]) * cross_tall,
+        }
+        items = {UP: level + 1, DOWN: depth - level, SIDE: depth}
+        ways = [way for way in (UP, DOWN, SIDE) if has[way]]
+
+        def drain(less):
+            for way in ways:
+                sent = span(rows[way] - less.get(way, 0))
+                bulk(sent, send_sem.at[way], rest_sem.at[0]).wait_send()
+
+        @pl.when((z == level) & ~source)
+        def _():
+            drain({})
+
+        if level < 2:
+
+            @pl.when((z == level) & source)
+            def _():
+                drain({DOWN if level else SIDE: chunks[RELIEF][5]})
 
         @pl.when(z == level)
         def _():
-            bulk(span(depth * tall - ends * cross_tall), send_sem.at[SIDE], rest_sem.at[0]).wait_send()
-            for way, rows, items in (
-                (UP, up_rows, level + 1),
-                (DOWN, down_rows, depth - level),
-            ):
-                if rows:
-                    bulk(span(rows), send_sem.at[way], rest_sem.at[0]).wait_send()
-                    bulk(
-                        gains.at[pl.ds(0, items)], gain_send.at[way], gain_rest.at[0]
-                    ).wait_send()
+            sent = gains.at[pl.ds(0, sum(items[way] for way in ways))]
+            bulk(sent, gain_send.at[0], gain_rest.at[0]).wait_send()
 
 
 def fused(size, tp_size, *args):
@@ -308,7 +389,8 @@
     ]
     outs.append(pltpu.VMEM((seats, norm_length), jnp.bfloat16))
     lengths = [t.shape[1] for t in (train_query, train_key, train_value)]
-    count = sum(len(cuts(length, n == 0)) for n, length in enumerate(lengths))
+    sizes = [rows for n, length in enumerate(lengths) for _, rows in cuts(length, n == 0)]
+    count = len(sizes)
     grant = VMEM_BYTES - 2 * (sum(t.shape[1] for t in (train_query, train_key, train_value)) * full)
     grant -= 2 * seats * norm_length
     vmem = pl.BlockSpec(memory_space=pltpu.VMEM)
@@ -319,17 +401,19 @@
         out_specs=[vmem] * 4,
         scratch_shapes=[pltpu.VMEM(a.shape, a.dtype) for a in args]
         + [
-            pltpu.VMEM((size, tp_size, 1, norm_length), jnp.float32),
+            pltpu.VMEM((2 * size, tp_size, 1, norm_length), jnp.float32),
             pltpu.SemaphoreType.DMA((11,)),
             pltpu.SemaphoreType.DMA((3,)),
             pltpu.SemaphoreType.DMA((size // 2, count)),
-            pltpu.SemaphoreType.DMA((count,)),
+            pltpu.SemaphoreType.DMA((len(crossed(sizes)),)),
             pltpu.SemaphoreType.DMA((1,)),
-            pltpu.SemaphoreType.DMA((3,)),
+            pltpu.SemaphoreType.DMA((1,)),
             pltpu.SemaphoreType.DMA((size // 2,)),
             pltpu.SemaphoreType.DMA((1,)),
-            pltpu.SemaphoreType.DMA((tp_size,)),
-            pltpu.SemaphoreType.DMA((tp_size,)),
+            pltpu.SemaphoreType.DMA((tp_size - 1,)),
+            pltpu.SemaphoreType.DMA((tp_size - 1,)),
+            pltpu.VMEM((SMALL_ROWS, train_query.shape[0]), jnp.bfloat16),
+            pltpu.SemaphoreType.DMA((3,)),
         ],
         compiler_params=pltpu.CompilerParams(
             collective_id=0, has_side_effects=True, vmem_limit_bytes=grant
@@ -396,7 +480,11 @@
         fits = (
             size % 2 == 0
             and size >= 4
-            and all(t.shape[0] % 128 == 0 and t.shape[1] % FIRST_ROWS == 0 for t in trains)
+            and tp_size > 1
+            and mesh.shape["job"] > 1
+            and SMALL_ROWS % (8 * size) == 0
+            and all(t.shape[0] % 128 == 0 and t.shape[1] % CHUNK_ROWS == 0 for t in trains)
+            and 2 * trains[0].shape[1] >= sum(t.shape[1] for t in trains)
             and args[9].shape[0] % 128 == 0
         )
         return fused(size, tp_size, *args) if fits else plain(*args)

time: 68.2 us -> 67.5 us (0.990)
  Pallas kernels: 67.4 us -> 66.7 us
    pallas_call x1, Pallas kernels: 64.7 us -> 64 us  [fused(): pl.pallas_call(functools.partial(kernel, size, tp_size), out_shape=outs,...]
where the time goes in v2:
time: 67.5 us; the launch traced here: 67.3 us
  Pallas kernels  66.7 us (99%)
    pallas_call x1, Pallas kernels, fused(): pl.pallas_call(functools.partial(kernel, size, tp_size), out_shape=outs,...  64 us
    pallas_call x1, Pallas kernels, store_out(): pl.pallas_call(store_kernel, out_shape=[jax.ShapeDtypeStruct(a.shape, a.d...  2.71 us

profile of v2, /device:TPU:0, one launch (start us, length us, event | category | flops | bytes accessed | tf_op | source)
XLA Modules:
  0.0 67.3 jit_solution(1857386262260981337)
XLA Ops:
  0.6 64.0 %shard_map.138 = (bf16[1024,2048]{1,0:T(8,128)(2,1)S(1)}, bf16[256,2048]{1,0:T(8,128)(2,1)S(1)}, bf16[256,2048]{1,0:T(8,128)(2,1)S(1)}, bf16[16,128]{1,0:T(8,128)(2,1)S(1)}) custom-call(bf16[256,1024]{1,0:T(8,128)(2,1)} %refs_0_.1, bf16[16,256]{1,0:T(8,128)(2,1)} %bitcast.6, bf16[16,1024]{1,0:T(8,128)(2,1)} %refs_2_.1, bf16[256,256]{1,0:T(8,128)(2,1)} %refs_3_.1, ...), custom_call_target="tpu_custom_call" | custom-call | tf_op jit(solution)/shard_map/pallas_call | solution.py:397
  64.6 2.7 %shard_map.139 = (bf16[1024,2048]{1,0:T(8,128)(2,1)}, bf16[256,2048]{1,0:T(8,128)(2,1)}, bf16[256,2048]{1,0:T(8,128)(2,1)}, bf16[16,128]{1,0:T(8,128)(2,1)}) custom-call(bf16[1024,2048]{1,0:T(8,128)(2,1)S(1)} %get-tuple-element.12.refs_0_, bf16[256,2048]{1,0:T(8,128)(2,1)S(1)} %get-tuple-element.13.refs_1_, bf16[256,2048]{1,0:T(8,128)(2,1)S(1)} %get-tuple-element.14.refs_2_, ...), custom_call_target="tpu_custom_call" | custom-call | tf_op jit(solution)/shard_map/pallas_call | solution.py:436

commit v3 on v2

--- a/solution.py
+++ b/solution.py
@@ -8,15 +8,16 @@
 from jax.sharding import PartitionSpec as P
 
 mix_rate = 0.5
-CHUNK_ROWS = 256
+CHUNK_ROWS = 512
+UNIT_ROWS = 256
 SMALL_ROWS = 128
-RELIEF = 1
+RELIEF = 0
 VMEM_BYTES = 67043328
 MESH = pl.DeviceIdType.MESH
 
 
 def cuts(length, first):
-    sizes = [SMALL_ROWS] * 2 if first else []
+    sizes = [SMALL_ROWS, CHUNK_ROWS - SMALL_ROWS] if first else []
     length -= sum(sizes)
     while length:
         sizes.append(min(length, CHUNK_ROWS))
@@ -25,6 +26,17 @@
     for rows in sizes:
         found.append((start, rows))
         start += rows
+    return found
+
+
+def units(chunks):
+    found = []
+    for c, (start, rows) in enumerate(chunks):
+        at = start
+        while at < start + rows:
+            step = SMALL_ROWS if len(found) < 2 else min(UNIT_ROWS, start + rows - at)
+            found.append((c, at, step))
+            at += step
     return found
 
 
@@ -58,7 +70,6 @@
     serve_value,
     serve_norm,
     gains,
-    load_sem,
     send_sem,
     line_sem,
     cross_sem,
@@ -71,9 +82,6 @@
     stage,
     stage_sem,
 ):
-    loads = [
-        pltpu.make_async_copy(g, h, load_sem.at[n]) for n, (g, h) in enumerate(zip(given, held))
-    ]
     (
         train_query,
         low_query,
@@ -130,9 +138,6 @@
     def _():
         greet({"job": 0})
 
-    for load in loads:
-        load.start()
-
     chunks = []
     for train, low, high, serve in (
         (train_query, low_query, high_query, serve_query),
@@ -142,28 +147,32 @@
         for start, rows in cuts(serve.shape[0], not chunks):
             chunks.append((train, low, high, serve, start, rows))
     count = len(chunks)
-    queries = sum(c[3] is serve_query for c in chunks)
+    parts = units([c[4:] for c in chunks])
+    queries = sum(chunks[c][3] is serve_query for c, _, _ in parts)
     crossings = crossed([c[5] for c in chunks])
     tall = sum(c[5] for c in chunks)
     cross_tall = sum(chunks[c][5] for c in crossings)
 
-    def piece(item, c):
+    def piece(item, c, part=None):
         if c == count:
             return gains.at[item]
         serve, start, rows = chunks[c][3:]
+        if part is not None:
+            _, start, rows = part
         return serve.at[pl.ds(start, rows), pl.ds(pl.multiple_of(item * width, 128), width)]
 
     def landing(item, c, way, own_side):
+        slot = item // 2 - 1 if way == DOWN else item // 2
         if c == count:
-            return gain_rest.at[0] if way == SIDE else gain_line.at[item // 2]
+            return gain_rest.at[0] if way == SIDE else gain_line.at[slot]
         if way != SIDE:
-            return line_sem.at[item // 2, c]
+            return line_sem.at[slot, c]
         if own_side and crossing(c):
             return cross_sem.at[crossings.index(c)]
         return rest_sem.at[0]
 
-    def copy(item, c, way, recv):
-        ref = piece(item, c)
+    def copy(item, c, way, recv, part=None):
+        ref = piece(item, c, part)
         return pltpu.make_async_remote_copy(
             src_ref=ref,
             dst_ref=ref,
@@ -173,11 +182,11 @@
             device_id_type=MESH,
         )
 
-    def send(item, c, way, own=False):
-        copy(item, c, way, landing(item, c, way, own)).start()
-
-    def arrive_line(item, c):
-        copy(item, c, UP, landing(item, c, UP, False)).wait_recv()
+    def send(item, c, way, own=False, part=None):
+        copy(item, c, way, landing(item, c, way, own), part).start()
+
+    def arrive_line(item, c, way):
+        copy(item, c, way, landing(item, c, way, False)).wait_recv()
 
     def bulk(ref, send, recv):
         return pltpu.make_async_remote_copy(
@@ -195,8 +204,9 @@
     def crossing(c):
         return c in crossings
 
-    def merge(c):
-        train, low, high, serve, start, length = chunks[c]
+    def merge(n):
+        c, start, length = parts[n]
+        train, low, high, serve = chunks[c][:4]
         rows = pl.ds(start, length)
         update = lax.dot_general(
             high[:, rows], low[...], (((0,), (0,)), ((), ())), preferred_element_type=jnp.float32
@@ -204,7 +214,7 @@
         fresh = train[:, rows].T.astype(jnp.float32) + mix_rate * update
         serve[rows, pl.ds(pl.multiple_of(me * width, 128), width)] = fresh.astype(jnp.bfloat16)
 
-    def send_own(c):
+    def send_own(c, part=None):
         down, across = has_down, True
         if c == RELIEF:
             down, across = has_down & ~(source & (me == 2)), ~(source & (me == 1))
@@ -215,15 +225,15 @@
 
         @pl.when(down)
         def _():
-            send(me, c, DOWN)
+            send(me, c, DOWN, part=part)
 
         @pl.when(has_up)
         def _():
-            send(me, c, UP)
+            send(me, c, UP, part=part)
 
         @pl.when(across)
         def _():
-            send(me, c, SIDE, own=True)
+            send(me, c, SIDE, own=True, part=part)
 
     def hand_over():
         return pltpu.make_async_remote_copy(
@@ -239,7 +249,7 @@
         return pltpu.make_async_remote_copy(
             src_ref=stage,
             dst_ref=piece(me, RELIEF),
-            send_sem=stage_sem.at[2],
+            send_sem=stage_sem.at[0],
             recv_sem=landing(me, RELIEF, way, True),
             device_id={"job": 0, "rows": 0},
             device_id_type=MESH,
@@ -255,23 +265,31 @@
             device_id_type=MESH,
         )
 
-    for n in (0, 1, 2, 9, 10):
-        loads[n].wait()
-    gains[pl.ds(me, 1), pl.ds(core, 1)] = (norm_train[...] + norm_step[...])[None, None]
-    merge(0)
-    merge(1)
-    expected = sum(e.astype(jnp.int32) for e in (has_up, has_down, source, helper))
-    pl.semaphore_wait(barrier, tp_size + expected)
-    for c in range(2, count + 2):
-        send_own(c - 2)
-        if c < count:
-            if c == queries:
-                for n in range(3, 9):
-                    loads[n].wait()
-            merge(c)
-        if c == 3:
-            for k in range(1, tp_size):
-                gain_copy(k).start()
+    def front(load_sem):
+        loads = [
+            pltpu.make_async_copy(g, h, load_sem.at[n]) for n, (g, h) in enumerate(zip(given, held))
+        ]
+        for load in loads:
+            load.start()
+        for n in (0, 1, 2, 9, 10):
+            loads[n].wait()
+        gains[pl.ds(me, 1), pl.ds(core, 1)] = (norm_train[...] + norm_step[...])[None, None]
+        merge(0)
+        merge(1)
+        expected = sum(e.astype(jnp.int32) for e in (has_up, has_down, source, helper))
+        pl.semaphore_wait(barrier, tp_size + expected)
+        for n in range(2, len(parts) + 2):
+            send_own(parts[n - 2][0], parts[n - 2])
+            if n < len(parts):
+                if n == queries:
+                    for m in range(3, 9):
+                        loads[m].wait()
+                merge(n)
+            if n == 3:
+                for k in range(1, tp_size):
+                    gain_copy(k).start()
+
+    pl.run_scoped(front, pltpu.SemaphoreType.DMA((len(given),)))
     for k in range(1, tp_size):
         gain_copy(k).wait_recv()
     send_own(count)
@@ -293,7 +311,7 @@
 
         @pl.when(z >= step)
         def _():
-            arrive_line(below, c)
+            arrive_line(below, c, UP)
 
             @pl.when(has_up)
             def _():
@@ -304,7 +322,7 @@
 
         @pl.when(z + step < depth)
         def _():
-            arrive_line(above, c)
+            arrive_line(above, c, DOWN)
 
             @pl.when(has_down)
             def _():
@@ -402,18 +420,17 @@
         scratch_shapes=[pltpu.VMEM(a.shape, a.dtype) for a in args]
         + [
             pltpu.VMEM((2 * size, tp_size, 1, norm_length), jnp.float32),
-            pltpu.SemaphoreType.DMA((11,)),
             pltpu.SemaphoreType.DMA((3,)),
-            pltpu.SemaphoreType.DMA((size // 2, count)),
+            pltpu.SemaphoreType.DMA((size // 2 - 1, count)),
             pltpu.SemaphoreType.DMA((len(crossed(sizes)),)),
             pltpu.SemaphoreType.DMA((1,)),
             pltpu.SemaphoreType.DMA((1,)),
-            pltpu.SemaphoreType.DMA((size // 2,)),
+            pltpu.SemaphoreType.DMA((size // 2 - 1,)),
             pltpu.SemaphoreType.DMA((1,)),
             pltpu.SemaphoreType.DMA((tp_size - 1,)),
             pltpu.SemaphoreType.DMA((tp_size - 1,)),
             pltpu.VMEM((SMALL_ROWS, train_query.shape[0]), jnp.bfloat16),
-            pltpu.SemaphoreType.DMA((3,)),
+            pltpu.SemaphoreType.DMA((2,)),
         ],
         compiler_params=pltpu.CompilerParams(
             collective_id=0, has_side_effects=True, vmem_limit_bytes=grant
@@ -483,7 +500,8 @@
             and tp_size > 1
             and mesh.shape["job"] > 1
             and SMALL_ROWS % (8 * size) == 0
-            and all(t.shape[0] % 128 == 0 and t.shape[1] % CHUNK_ROWS == 0 for t in trains)
+            and all(t.shape[0] % 128 == 0 and t.shape[1] % SMALL_ROWS == 0 for t in trains)
+            and trains[0].shape[1] >= 2 * CHUNK_ROWS
             and 2 * trains[0].shape[1] >= sum(t.shape[1] for t in trains)
             and args[9].shape[0] % 128 == 0
         )

time: 67.5 us -> 67.2 us (level)
  no operation moved by 1% of the time
where the time goes in v3:
time: 67.2 us; the launch traced here: 67.1 us
  Pallas kernels  66.5 us (99%)
    pallas_call x1, Pallas kernels, fused(): pl.pallas_call(functools.partial(kernel, size, tp_size), out_shape=outs,...  63.8 us
    pallas_call x1, Pallas kernels, store_out(): pl.pallas_call(store_kernel, out_shape=[jax.ShapeDtypeStruct(a.shape, a.d...  2.71 us

profile of v3, /device:TPU:0, one launch (start us, length us, event | category | flops | bytes accessed | tf_op | source)
XLA Modules:
  0.0 67.1 jit_solution(4897123776037528240)
XLA Ops:
  0.6 63.8 %shard_map.138 = (bf16[1024,2048]{1,0:T(8,128)(2,1)S(1)}, bf16[256,2048]{1,0:T(8,128)(2,1)S(1)}, bf16[256,2048]{1,0:T(8,128)(2,1)S(1)}, bf16[16,128]{1,0:T(8,128)(2,1)S(1)}) custom-call(bf16[256,1024]{1,0:T(8,128)(2,1)} %refs_0_.1, bf16[16,256]{1,0:T(8,128)(2,1)} %bitcast.6, bf16[16,1024]{1,0:T(8,128)(2,1)} %refs_2_.1, bf16[256,256]{1,0:T(8,128)(2,1)} %refs_3_.1, ...), custom_call_target="tpu_custom_call" | custom-call | tf_op jit(solution)/shard_map/pallas_call | solution.py:415
  64.4 2.7 %shard_map.139 = (bf16[1024,2048]{1,0:T(8,128)(2,1)}, bf16[256,2048]{1,0:T(8,128)(2,1)}, bf16[256,2048]{1,0:T(8,128)(2,1)}, bf16[16,128]{1,0:T(8,128)(2,1)}) custom-call(bf16[1024,2048]{1,0:T(8,128)(2,1)S(1)} %get-tuple-element.12.refs_0_, bf16[256,2048]{1,0:T(8,128)(2,1)S(1)} %get-tuple-element.13.refs_1_, bf16[256,2048]{1,0:T(8,128)(2,1)S(1)} %get-tuple-element.14.refs_2_, ...), custom_call_target="tpu_custom_call" | custom-call | tf_op jit(solution)/shard_map/pallas_call | solution.py:453

commit v4 on v3

--- a/solution.py
+++ b/solution.py
@@ -12,6 +12,7 @@
 UNIT_ROWS = 256
 SMALL_ROWS = 128
 RELIEF = 0
+LOAD_SEMS = (0, 1, 2, 3, 3, 3, 3, 3, 3, 4, 4)
 VMEM_BYTES = 67043328
 MESH = pl.DeviceIdType.MESH
 
@@ -70,6 +71,7 @@
     serve_value,
     serve_norm,
     gains,
+    load_sem,
     send_sem,
     line_sem,
     cross_sem,
@@ -82,6 +84,10 @@
     stage,
     stage_sem,
 ):
+    loads = [
+        pltpu.make_async_copy(g, h, load_sem.at[LOAD_SEMS[n]])
+        for n, (g, h) in enumerate(zip(given, held))
+    ]
     (
         train_query,
         low_query,
@@ -138,6 +144,9 @@
     def _():
         greet({"job": 0})
 
+    for load in loads:
+        load.start()
+
     chunks = []
     for train, low, high, serve in (
         (train_query, low_query, high_query, serve_query),
@@ -265,31 +274,25 @@
             device_id_type=MESH,
         )
 
-    def front(load_sem):
-        loads = [
-            pltpu.make_async_copy(g, h, load_sem.at[n]) for n, (g, h) in enumerate(zip(given, held))
-        ]
-        for load in loads:
-            load.start()
-        for n in (0, 1, 2, 9, 10):
-            loads[n].wait()
-        gains[pl.ds(me, 1), pl.ds(core, 1)] = (norm_train[...] + norm_step[...])[None, None]
-        merge(0)
-        merge(1)
-        expected = sum(e.astype(jnp.int32) for e in (has_up, has_down, source, helper))
-        pl.semaphore_wait(barrier, tp_size + expected)
-        for n in range(2, len(parts) + 2):
-            send_own(parts[n - 2][0], parts[n - 2])
-            if n < len(parts):
-                if n == queries:
-                    for m in range(3, 9):
-                        loads[m].wait()
-                merge(n)
-            if n == 3:
-                for k in range(1, tp_size):
-                    gain_copy(k).start()
-
-    pl.run_scoped(front, pltpu.SemaphoreType.DMA((len(given),)))
+    for n in (0, 1, 2):
+        loads[n].wait()
+    bulk(gains.at[0], pair_send.at[0], load_sem.at[4]).wait_recv()
+    gains[pl.ds(me, 1), pl.ds(core, 1)] = (norm_train[...] + norm_step[...])[None, None]
+    merge(0)
+    merge(1)
+    expected = sum(e.astype(jnp.int32) for e in (has_up, has_down, source, helper))
+    pl.semaphore_wait(barrier, tp_size + expected)
+    for n in range(2, len(parts) + 2):
+        send_own(parts[n - 2][0], parts[n - 2])
+        if n < len(parts):
+            if n == queries:
+                loaded = sum(h.shape[0] * h.shape[1] for h in held[3:9]) // (size * width)
+                whole = serve_query.at[pl.ds(0, loaded), :]
+                bulk(whole, pair_send.at[0], load_sem.at[3]).wait_recv()
+            merge(n)
+        if n == 3:
+            for k in range(1, tp_size):
+                gain_copy(k).start()
     for k in range(1, tp_size):
         gain_copy(k).wait_recv()
     send_own(count)
@@ -420,6 +423,7 @@
         scratch_shapes=[pltpu.VMEM(a.shape, a.dtype) for a in args]
         + [
             pltpu.VMEM((2 * size, tp_size, 1, norm_length), jnp.float32),
+            pltpu.SemaphoreType.DMA((max(LOAD_SEMS) + 1,)),
             pltpu.SemaphoreType.DMA((3,)),
             pltpu.SemaphoreType.DMA((size // 2 - 1, count)),
             pltpu.SemaphoreType.DMA((len(crossed(sizes)),)),
@@ -497,13 +501,14 @@
         fits = (
             size % 2 == 0
             and size >= 4
-            and tp_size > 1
+            and tp_size == 2
             and mesh.shape["job"] > 1
             and SMALL_ROWS % (8 * size) == 0
             and all(t.shape[0] % 128 == 0 and t.shape[1] % SMALL_ROWS == 0 for t in trains)
             and trains[0].shape[1] >= 2 * CHUNK_ROWS
             and 2 * trains[0].shape[1] >= sum(t.shape[1] for t in trains)
             and args[9].shape[0] % 128 == 0
+            and sum(a.size for a in args[3:9]) % (8 * size * trains[0].shape[0]) == 0
         )
         return fused(size, tp_size, *args) if fits else plain(*args)
 

time: 67.2 us -> 67.3 us (level)
  no operation moved by 1% of the time
where the time goes in v4:
time: 67.3 us; the launch traced here: 67.2 us
  Pallas kernels  66.5 us (99%)
    pallas_call x1, Pallas kernels, fused(): pl.pallas_call(functools.partial(kernel, size, tp_size), out_shape=outs,...  63.8 us
    pallas_call x1, Pallas kernels, store_out(): pl.pallas_call(store_kernel, out_shape=[jax.ShapeDtypeStruct(a.shape, a.d...  2.71 us

profile of v4, /device:TPU:0, one launch (start us, length us, event | category | flops | bytes accessed | tf_op | source)
XLA Modules:
  0.0 67.2 jit_solution(11437052578330460667)
XLA Ops:
  0.6 63.8 %shard_map.138 = (bf16[1024,2048]{1,0:T(8,128)(2,1)S(1)}, bf16[256,2048]{1,0:T(8,128)(2,1)S(1)}, bf16[256,2048]{1,0:T(8,128)(2,1)S(1)}, bf16[16,128]{1,0:T(8,128)(2,1)S(1)}) custom-call(bf16[256,1024]{1,0:T(8,128)(2,1)} %refs_0_.1, bf16[16,256]{1,0:T(8,128)(2,1)} %bitcast.6, bf16[16,1024]{1,0:T(8,128)(2,1)} %refs_2_.1, bf16[256,256]{1,0:T(8,128)(2,1)} %refs_3_.1, ...), custom_call_target="tpu_custom_call" | custom-call | tf_op jit(solution)/shard_map/pallas_call | solution.py:418
  64.4 2.7 %shard_map.139 = (bf16[1024,2048]{1,0:T(8,128)(2,1)}, bf16[256,2048]{1,0:T(8,128)(2,1)}, bf16[256,2048]{1,0:T(8,128)(2,1)}, bf16[16,128]{1,0:T(8,128)(2,1)}) custom-call(bf16[1024,2048]{1,0:T(8,128)(2,1)S(1)} %get-tuple-element.12.refs_0_, bf16[256,2048]{1,0:T(8,128)(2,1)S(1)} %get-tuple-element.13.refs_1_, bf16[256,2048]{1,0:T(8,128)(2,1)S(1)} %get-tuple-element.14.refs_2_, ...), custom_call_target="tpu_custom_call" | custom-call | tf_op jit(solution)/shard_map/pallas_call | solution.py:457

commit v5 on v4

--- a/solution.py
+++ b/solution.py
@@ -12,7 +12,7 @@
 UNIT_ROWS = 256
 SMALL_ROWS = 128
 RELIEF = 0
-LOAD_SEMS = (0, 1, 2, 3, 3, 3, 3, 3, 3, 4, 4)
+LOAD_SEMS = (0, 0, 0, 1, 1, 1, 1, 1, 1, 2, 2)
 VMEM_BYTES = 67043328
 MESH = pl.DeviceIdType.MESH
 
@@ -177,7 +177,7 @@
         if way != SIDE:
             return line_sem.at[slot, c]
         if own_side and crossing(c):
-            return cross_sem.at[crossings.index(c)]
+            return cross_sem.at[0]
         return rest_sem.at[0]
 
     def copy(item, c, way, recv, part=None):
@@ -274,9 +274,10 @@
             device_id_type=MESH,
         )
 
-    for n in (0, 1, 2):
-        loads[n].wait()
-    bulk(gains.at[0], pair_send.at[0], load_sem.at[4]).wait_recv()
+    loaded = sum(h.shape[0] * h.shape[1] for h in held[:3]) // (2 * width)
+    block = serve_query.at[pl.ds(0, loaded), pl.ds(0, 2 * width)]
+    bulk(block, pair_send.at[0], load_sem.at[0]).wait_recv()
+    bulk(gains.at[0], pair_send.at[0], load_sem.at[2]).wait_recv()
     gains[pl.ds(me, 1), pl.ds(core, 1)] = (norm_train[...] + norm_step[...])[None, None]
     merge(0)
     merge(1)
@@ -288,7 +289,7 @@
             if n == queries:
                 loaded = sum(h.shape[0] * h.shape[1] for h in held[3:9]) // (size * width)
                 whole = serve_query.at[pl.ds(0, loaded), :]
-                bulk(whole, pair_send.at[0], load_sem.at[3]).wait_recv()
+                bulk(whole, pair_send.at[0], load_sem.at[1]).wait_recv()
             merge(n)
         if n == 3:
             for k in range(1, tp_size):
@@ -335,8 +336,6 @@
                 send(above, c, SIDE)
 
     def cross(c):
-        copy(side, c, SIDE, landing(side, c, SIDE, True)).wait_recv()
-
         @pl.when(has_down)
         def _():
             copy(side, c, DOWN, rest_sem.at[0]).start()
@@ -350,6 +349,7 @@
         for c in order:
             pass_on(step, c)
         if step == max(1, depth - 2):
+            bulk(span(cross_tall), send_sem.at[SIDE], cross_sem.at[0]).wait_recv()
             for c in crossings:
                 cross(c)
 
@@ -426,7 +426,7 @@
             pltpu.SemaphoreType.DMA((max(LOAD_SEMS) + 1,)),
             pltpu.SemaphoreType.DMA((3,)),
             pltpu.SemaphoreType.DMA((size // 2 - 1, count)),
-            pltpu.SemaphoreType.DMA((len(crossed(sizes)),)),
+            pltpu.SemaphoreType.DMA((1,)),
             pltpu.SemaphoreType.DMA((1,)),
             pltpu.SemaphoreType.DMA((1,)),
             pltpu.SemaphoreType.DMA((size // 2 - 1,)),
@@ -508,6 +508,8 @@
             and trains[0].shape[1] >= 2 * CHUNK_ROWS
             and 2 * trains[0].shape[1] >= sum(t.shape[1] for t in trains)
             and args[9].shape[0] % 128 == 0
+            and sum(a.size for a in args[:3]) % (16 * trains[0].shape[0]) == 0
+            and sum(a.size for a in args[:3]) <= 2 * trains[0].size
             and sum(a.size for a in args[3:9]) % (8 * size * trains[0].shape[0]) == 0
         )
         return fused(size, tp_size, *args) if fits else plain(*args)

time: 67.3 us -> 67.3 us (level)
  no operation moved by 1% of the time
where the time goes in v5:
time: 67.3 us; the launch traced here: 67.1 us
  Pallas kernels  66.5 us (99%)
    pallas_call x1, Pallas kernels, fused(): pl.pallas_call(functools.partial(kernel, size, tp_size), out_shape=outs,...  63.8 us
    pallas_call x1, Pallas kernels, store_out(): pl.pallas_call(store_kernel, out_shape=[jax.ShapeDtypeStruct(a.shape, a.d...  2.71 us

profile of v5, /device:TPU:0, one launch (start us, length us, event | category | flops | bytes accessed | tf_op | source)
XLA Modules:
  0.0 67.1 jit_solution(12968781245572360623)
XLA Ops:
  0.6 63.8 %shard_map.138 = (bf16[1024,2048]{1,0:T(8,128)(2,1)S(1)}, bf16[256,2048]{1,0:T(8,128)(2,1)S(1)}, bf16[256,2048]{1,0:T(8,128)(2,1)S(1)}, bf16[16,128]{1,0:T(8,128)(2,1)S(1)}) custom-call(bf16[256,1024]{1,0:T(8,128)(2,1)} %refs_0_.1, bf16[16,256]{1,0:T(8,128)(2,1)} %bitcast.6, bf16[16,1024]{1,0:T(8,128)(2,1)} %refs_2_.1, bf16[256,256]{1,0:T(8,128)(2,1)} %refs_3_.1, ...), custom_call_target="tpu_custom_call" | custom-call | tf_op jit(solution)/shard_map/pallas_call | solution.py:418
  64.4 2.7 %shard_map.139 = (bf16[1024,2048]{1,0:T(8,128)(2,1)}, bf16[256,2048]{1,0:T(8,128)(2,1)}, bf16[256,2048]{1,0:T(8,128)(2,1)}, bf16[16,128]{1,0:T(8,128)(2,1)}) custom-call(bf16[1024,2048]{1,0:T(8,128)(2,1)S(1)} %get-tuple-element.12.refs_0_, bf16[256,2048]{1,0:T(8,128)(2,1)S(1)} %get-tuple-element.13.refs_1_, bf16[256,2048]{1,0:T(8,128)(2,1)S(1)} %get-tuple-element.14.refs_2_, ...), custom_call_target="tpu_custom_call" | custom-call | tf_op jit(solution)/shard_map/pallas_call | solution.py:457
